TPU v7x, 256 devices: a whole 4x4x8 slice. The times are simulated.
256 devices in a mesh: ctx: 8 (over z), vocab: 32 (over y, x, core).
Axes of the slice: x: 4, y: 4, z: 8, core: 2. Of those that a mesh axis runs over, the one named last changes fastest.
Arguments:
- hidden: bfloat16 [16, 128, 4096], P(None, 'ctx', 'vocab'), may hold values from -6 to 6
- head_weight: bfloat16 [4096, 128256], P(None, ('ctx', 'vocab')), may hold values from -0.09375 to 0.09375
- token_ids: int32 [16, 128], P(None, 'ctx'), may hold values from 0 to 128255
- response_mask: int32 [16, 128], P(None, 'ctx'), may hold values 0 or 1
- pair_order: int32 [16], replicated, may hold values from 0 to 15, each once
- frozen_logprob: float32 [16], replicated, may hold values from -40 to 40
Outputs:
- pair_loss: float32 [], replicated
- margins: float32 [8], replicated
- head_grad: bfloat16 [4096, 128256], P(None, ('ctx', 'vocab'))
- spread_grad: bfloat16 [4096, 128256], P(None, ('ctx', 'vocab'))
Inputs may be any that keep to these rules, and one draw needn't show every extreme that they name: `token_ids`: token ids lie in 0 to 128255. `response_mask`: mask entries are 0 or 1. pair_order names every sequence exactly once; entry p is the chosen sequence of pair p and entry 8 + p the rejected one.
All inputs are finite; a program needn't handle non-finite values.
Results may differ from a plain program's by a relative error of at most 0.0015.
Values may be sent and summed in bfloat16 or wider, within the bound.
No kernel may reach another device: no remote copies, remote signals or barrier semaphores. Data moves between devices by JAX's collectives and lax.ppermute only.
A program may use at most 128 MiB of HBM per device.

v0:
```python
import jax
import jax.numpy as jnp
from jax import lax
from jax.sharding import Mesh
from jax.sharding import PartitionSpec as P

V = 128256
VOCAB = ("vocab_0", "vocab_1", "vocab_2")
CTX_VOCAB = ("ctx", "vocab_0", "vocab_1", "vocab_2")


strength = 0.1
loss_scale = 256.0


def laid_out(pieces, dim):
    pieces = jnp.moveaxis(pieces, 0, dim)
    lengths = pieces.shape
    return pieces.reshape(*lengths[:dim], lengths[dim] * lengths[dim + 1], *lengths[dim + 2 :])


def gather_packed(arrays, axis, dims):
    flat = jnp.concatenate([a.reshape(-1) for a in arrays])
    lines, at, finished = lax.all_gather(flat, axis), 0, []
    for a, dim in zip(arrays, dims):
        pieces = lines[:, at : at + a.size].reshape(-1, *a.shape)
        finished.append(laid_out(pieces, dim))
        at += a.size
    return tuple(finished)


def by_axis(shard, axes):
    for axis in axes:
        shard = lax.pmax(shard, axis)
    return shard


def by_axis_2(shard, axes):
    for axis in axes:
        shard = lax.psum(shard, axis)
    return shard


def contract_rows(block_rows, both_logits):
    return lax.dot_general(
        block_rows, both_logits, (((0,), (0,)), ((), ())), preferred_element_type=jnp.float32
    )


def shards(hidden, head_weight, token_ids, response_mask, pair_order, frozen_logprob):
    seq_rows = lax.all_gather(hidden, "ctx", axis=1, tiled=True)
    ids_all, mask_all = gather_packed((token_ids, response_mask), "ctx", (1, 1))
    token_rows = seq_rows.reshape(seq_rows.shape[0] * seq_rows.shape[1], seq_rows.shape[2])
    shard_width = head_weight.shape[1]
    whole_rows = lax.all_gather(token_rows, VOCAB, axis=1, tiled=True)
    logits = jnp.dot(whole_rows, head_weight, preferred_element_type=jnp.float32)
    offset = lax.axis_index(CTX_VOCAB) * shard_width
    local_ids = ids_all.reshape(-1) - offset
    columns = jnp.arange(shard_width).astype(jnp.int32)
    onehot = (columns[None, :] == local_ids[:, None]).astype(jnp.float32)
    picked_part = jnp.sum(onehot * logits, axis=1)
    peak_part = jnp.max(logits, axis=1)
    row_peak = by_axis(peak_part, CTX_VOCAB)
    exp_sums = jnp.sum(jnp.exp(logits - row_peak[:, None]), axis=1)
    sum_total, picked = (by_axis_2(exp_sums, CTX_VOCAB), by_axis_2(picked_part, CTX_VOCAB))
    log_norm = row_peak + jnp.log(sum_total)
    mask_flat = mask_all.reshape(-1).astype(jnp.float32)
    seq_count = ids_all.shape[0]
    policy = jnp.sum(((picked - log_norm) * mask_flat).reshape(seq_count, ids_all.shape[1]), axis=1)
    log_ratio = policy - frozen_logprob
    pair_count = pair_order.shape[0] // 2
    chosen = pair_order[:pair_count]
    rejected = pair_order[pair_count:]
    margins = strength * (log_ratio[chosen] - log_ratio[rejected])
    pair_loss = jnp.mean(jax.nn.softplus(-margins))
    weight = -loss_scale * strength * jax.nn.sigmoid(-margins) / pair_count
    seq_coef = jnp.zeros((seq_count,), jnp.float32).at[chosen].set(weight).at[rejected].set(-weight)
    token_coef = (seq_coef[:, None] * mask_all.astype(jnp.float32)).reshape(-1)
    probabilities = jnp.exp(logits - log_norm[:, None])
    grad_logits = (token_coef[:, None] * (onehot - probabilities)).astype(jnp.bfloat16)
    spread_logits = (V / 64.0 * token_coef[:, None] * probabilities).astype(jnp.bfloat16)
    both_logits = jnp.concatenate([grad_logits, spread_logits], axis=1)
    both_grads = contract_rows(whole_rows, both_logits)
    head_grad = both_grads[:, :shard_width].astype(jnp.bfloat16)
    spread_grad = both_grads[:, shard_width:].astype(jnp.bfloat16)
    return (pair_loss, margins, head_grad, spread_grad)


def solution(mesh):
    split = Mesh(
        mesh.devices.reshape(mesh.shape["ctx"], 4, 4, 2), ("ctx", "vocab_0", "vocab_1", "vocab_2")
    )
    placed = (P(None, "ctx", VOCAB), P(None, CTX_VOCAB), P(None, "ctx"), P(None, "ctx"), P(), P())
    return jax.shard_map(
        shards,
        mesh=split,
        in_specs=placed,
        out_specs=(P(), P(), P(None, CTX_VOCAB), P(None, CTX_VOCAB)),
        check_vma=False,
    )
```

profile of v0, /device:TPU:1, one launch (start us, length us, event | category | flops | bytes accessed | tf_op | source)
XLA Modules:
  0.0 281.2 jit_solution(17380326910799111413)
XLA Ops:
  7.2 26.5 %all_gather.14 = bf16[16,128,128]{2,1,0:T(8,128)(2,1)} all-gather(bf16[16,16,128]{2,1,0:T(8,128)(2,1)} %param.6), channel_id=1, replica_groups=mesh['ctx'=8,'vocab_0'=4,'vocab_1'=4,'vocab_2'=2] {'ctx'}, dimensions={1}, use_global_device_ids=true | all-gather | bytes 589824 | tf_op jit(solution)/shard_map/all_gather | solution.py:51
  33.7 0.8 reshape.60
  34.5 0.8 reshape.61
  35.3 18.1 %all-gather.1 = s32[8,1,512]{2,1,0:T(1,128)S(1)} all-gather(s32[1,1,512]{2,1,0:T(1,128)S(1)} %bitcast.21), channel_id=2, replica_groups=mesh['ctx'=8,'vocab_0'=4,'vocab_1'=4,'vocab_2'=2] {'ctx'}, dimensions={0}, use_global_device_ids=true | all-gather | bytes 18432 | tf_op jit(solution)/shard_map/all_gather | solution.py:24
  53.8 0.8 compare_select_fusion.1
  54.6 68.8 %all-gather.4.cloned.1.call-done = bf16[2048,4096]{1,0:T(8,128)(2,1)} async-done(((bf16[2048,128]{1,0:T(8,128)(2,1)}), bf16[2048,4096]{1,0:T(8,128)(2,1)}) %all-gather.4.cloned.1.call-update) | async-done | bytes 16777232 | tf_op jit(solution)/shard_map/all_gather | solution.py:55
  123.5 14.8 %fusion.9 = (f32[2048]{0:T(1024)S(1)}, f32[2048,501]{0,1:T(8,128)}) fusion(bf16[2048,4096]{1,0:T(8,128)(2,1)} %all-gather.4.cloned.1.call-done, bf16[4096,501]{0,1:T(8,128)(2,1)} %param.7), kind=kOutput, calls=%fused_computation.35 | convolution fusion | flops 8406409216 | bytes 24993792 | tf_op jit(solution)/shard_map/dot_general | solution.py:56
  138.3 14.1 %pmax.28 = f32[2048]{0:T(1024)S(1)} all-reduce(f32[2048]{0:T(1024)S(1)} %get-tuple-element.29), channel_id=1, replica_groups=mesh['ctx'=8,'vocab_0'=4,'vocab_1'=4,'vocab_2'=2] {'ctx'}, use_global_device_ids=true, to_apply=%region_6.0 | all-reduce | flops 2048 | bytes 16384 | tf_op jit(solution)/shard_map/pmax | solution.py:34
  152.3 8.2 %pmax.29 = f32[2048]{0:T(1024)S(1)} all-reduce(f32[2048]{0:T(1024)S(1)} %pmax.28), channel_id=1, replica_groups=mesh['ctx'=8,'vocab_0'=4,'vocab_1'=4,'vocab_2'=2] {'vocab_0'}, use_global_device_ids=true, to_apply=%region_7.0 | all-reduce | flops 2048 | bytes 16384 | tf_op jit(solution)/shard_map/pmax | solution.py:34
  160.6 7.4 %pmax.30 = f32[2048]{0:T(1024)S(1)} all-reduce(f32[2048]{0:T(1024)S(1)} %pmax.29), channel_id=1, replica_groups=mesh['ctx'=8,'vocab_0'=4,'vocab_1'=4,'vocab_2'=2] {'vocab_1'}, use_global_device_ids=true, to_apply=%region_8.0 | all-reduce | flops 2048 | bytes 16384 | tf_op jit(solution)/shard_map/pmax | solution.py:34
  167.9 10.1 %pmax.31 = f32[2048]{0:T(1024)S(1)} all-reduce(f32[2048]{0:T(1024)S(1)} %pmax.30), channel_id=1, replica_groups=mesh['ctx'=8,'vocab_0'=4,'vocab_1'=4,'vocab_2'=2] {'vocab_2'}, use_global_device_ids=true, to_apply=%region_9.0 | all-reduce | flops 2048 | bytes 16384 | tf_op jit(solution)/shard_map/pmax | solution.py:34
  178.0 3.3 %exponential_reduce_fusion = (f32[2048]{0:T(1024)S(1)}, f32[2048]{0:T(1024)S(1)}) fusion(f32[2048,501]{0,1:T(8,128)} %get-tuple-element.30, f32[2048]{0:T(1024)S(1)} %pmax.31, s32[2048]{0:T(1024)S(1)} %sub.51), kind=kLoop, calls=%fused_computation.11 | loop fusion | flops 5126144 | bytes 4136960 | tf_op jit(solution)/shard_map/reduce_sum | solution.py:64
  181.3 20.5 %all-reduce = (f32[2048]{0:T(1024)S(1)}, f32[2048]{0:T(1024)S(1)}) all-reduce(f32[2048]{0:T(1024)S(1)} %get-tuple-element.5, f32[2048]{0:T(1024)S(1)} %get-tuple-element.4), channel_id=1, replica_groups=mesh['ctx'=8,'vocab_0'=4,'vocab_1'=4,'vocab_2'=2] {'ctx'}, use_global_device_ids=true, to_apply=%region_1.0 | all-reduce | flops 4096 | bytes 32768 | tf_op jit(solution)/shard_map/psum | solution.py:40
  201.8 10.8 %all-reduce.2 = (f32[2048]{0:T(1024)S(1)}, f32[2048]{0:T(1024)S(1)}) all-reduce(f32[2048]{0:T(1024)S(1)} %get-tuple-element.6, f32[2048]{0:T(1024)S(1)} %get-tuple-element.7), channel_id=1, replica_groups=mesh['ctx'=8,'vocab_0'=4,'vocab_1'=4,'vocab_2'=2] {'vocab_0'}, use_global_device_ids=true, to_apply=%region_2.0 | all-reduce | flops 4096 | bytes 32768 | tf_op jit(solution)/shard_map/psum | solution.py:40
  212.6 10.8 %all-reduce.1 = (f32[2048]{0:T(1024)S(1)}, f32[2048]{0:T(1024)S(1)}) all-reduce(f32[2048]{0:T(1024)S(1)} %get-tuple-element.10, f32[2048]{0:T(1024)S(1)} %get-tuple-element.11), channel_id=1, replica_groups=mesh['ctx'=8,'vocab_0'=4,'vocab_1'=4,'vocab_2'=2] {'vocab_1'}, use_global_device_ids=true, to_apply=%region_3.0 | all-reduce | flops 4096 | bytes 32768 | tf_op jit(solution)/shard_map/psum | solution.py:40
  223.5 17.9 %all-reduce.3 = (f32[2048]{0:T(1024)S(1)}, f32[2048]{0:T(1024)S(1)}) all-reduce(f32[2048]{0:T(1024)S(1)} %get-tuple-element.8, f32[2048]{0:T(1024)S(1)} %get-tuple-element.9), channel_id=1, replica_groups=mesh['ctx'=8,'vocab_0'=4,'vocab_1'=4,'vocab_2'=2] {'vocab_2'}, use_global_device_ids=true, to_apply=%region_4.0 | all-reduce | flops 4096 | bytes 32768 | tf_op jit(solution)/shard_map/psum | solution.py:40
  241.6 0.6 gather_fusion.1
  242.2 0.6 gather_fusion
  242.9 0.6 scatter_custom_fusion
  243.5 0.8 scatter_fusion
  244.3 3.5 %multiply_convert_fusion.1 = (bf16[2048,501]{0,1:T(8,128)(2,1)S(1)}, bf16[2048,501]{0,1:T(8,128)(2,1)S(1)}) fusion(f32[2048,501]{0,1:T(8,128)} %get-tuple-element.30, f32[2048]{0:T(1024)S(1)} %get-tuple-element.20, f32[2048]{0:T(1024)S(1)} %get-tuple-element.15, s32[2048]{0:T(1024)S(1)} %sub.51, f32[2048]{0:T(1024)S(1)} %get-tuple-element.14), kind=kLoop, calls=%fused_computation.9 | loop fusion | flops 8208384 | bytes 8241152 | tf_op jit(solution)/shard_map/convert_element_type | solution.py:80
  247.9 20.1 %convert_bitcast_fusion = bf16[4096,1002]{0,1:T(8,128)(2,1)S(1)} fusion(bf16[2048,4096]{1,0:T(8,128)(2,1)} %all-gather.4.cloned.1.call-done, bf16[2048,501]{0,1:T(8,128)(2,1)S(1)} %get-tuple-element.24, bf16[2048,501]{0,1:T(8,128)(2,1)S(1)} %get-tuple-element.23), kind=kOutput, calls=%fused_computation.4 | convolution fusion | flops 16823083008 | bytes 29089792 | tf_op jit(solution)/shard_map/dot_general | solution.py:45
  267.9 4.0 %fusion.8 = (bf16[4096,501]{0,1:T(8,128)(2,1)}, bf16[4096,501]{0,1:T(8,128)(2,1)}) fusion(bf16[4096,1002]{0,1:T(8,128)(2,1)S(1)} %convert_bitcast_fusion), kind=kLoop, calls=%fused_computation.34 | loop fusion | bytes 16416768 | tf_op jit(solution)/shard_map/slice | solution.py:85
  272.0 0.6 fusion.3
  (20 shorter events, 0.7 us)
Async XLA Ops:
  7.2 116.3 %all-gather.4.cloned.1.call-start = ((), (), s32[]{:S(2)}) async-start(), calls=%async_computation | async-start | bytes 17301504 | tf_op jit(solution)/shard_map/all_gather | solution.py:55
  138.3 103.3 %copy-start.1 = (f32[16]{0:T(128)S(1)}, f32[16]{0:T(128)}, u32[]{:S(2)}) copy-start(f32[16]{0:T(128)} %param.11) | copy-start | bytes 196
  242.9 29.1 %copy-start = (f32[8]{0:T(128)}, f32[8]{0:T(128)S(1)}, u32[]{:S(2)}) copy-start(f32[8]{0:T(128)S(1)} %get-tuple-element.18) | copy-start | bytes 100
Sparse Core Ops, SparseCore 0:
  33.8 89.5 all-gather.3
where the time goes:
time: 282 us; the launch traced here: 281 us
  blocking collectives  144 us (51%)
  waiting for transfers between devices  68.8 us (24%)
  matrix products  34.9 us (12%)
  between operations  15.9 us (6%)
  local copies, waits for them, and re-layouts  8.6 us (3%)
  other arithmetic  8.44 us (3%)
    all_gather x1, waiting for transfers between devices, shards(): whole_rows = lax.all_gather(token_rows, VOCAB, axis=1, tiled=True)  68.8 us
    psum x4, blocking collectives, by_axis_2(): shard = lax.psum(shard, axis)  60.1 us
    pmax x4, blocking collectives, by_axis(): shard = lax.pmax(shard, axis)  39.7 us
    all_gather x1, blocking collectives, shards(): seq_rows = lax.all_gather(hidden, 'ctx', axis=1, tiled=True)  26.5 us
    dot_general x1, matrix products, contract_rows(): lax.dot_general(block_rows, both_logits, (((0,), (0,)), ((), ())), prefer...  20.1 us
    all_gather x1, blocking collectives, gather_packed(): lines, at, finished = (lax.all_gather(flat, axis), 0, [])  18.1 us
    dot_general x1, matrix products, shards(): jnp.dot(whole_rows, head_weight, preferred_element_type=jnp.float32)  14.8 us
  transfers between devices with their start and end apart: 1, of which 1 were waited for; matrix products, arithmetic and copies ran while one was open for 1% of the time, Pallas kernels for 0%

commit v1 on v0

v1 whole, which is shorter than its diff:
```python
import jax
import jax.numpy as jnp
from jax import lax
from jax.sharding import Mesh
from jax.sharding import PartitionSpec as P

V = 128256
VOCAB = ("vocab_0", "vocab_1", "vocab_2")
CTX_VOCAB = ("ctx", "vocab_0", "vocab_1", "vocab_2")


strength = 0.1
loss_scale = 256.0


def to_planes(token_ids, response_mask):
    planes = jnp.stack([token_ids & 255, (token_ids >> 8) & 255, token_ids >> 16, response_mask])
    return planes.astype(jnp.bfloat16).reshape(-1, 128)


def from_planes(planes):
    low, mid, high, mask = planes
    ids = low.astype(jnp.int32) + 256 * mid.astype(jnp.int32) + 65536 * high.astype(jnp.int32)
    return ids, mask.astype(jnp.float32)


def exchange(lse, picked, axes, count):
    block = jnp.concatenate([lse.reshape(-1), picked, jnp.zeros((112,), jnp.float32)]).reshape(-1, 128)
    lines = lax.all_to_all(
        jnp.broadcast_to(block[None], (count, *block.shape)), axes, 0, 0, tiled=True
    )
    lines = lines.reshape(count, -1)
    parts = lines[:, : lse.size]
    peak = jnp.max(parts, axis=0)
    total = peak + jnp.log(jnp.sum(jnp.exp(parts - peak), axis=0))
    return total, jnp.sum(lines[:, lse.size : lse.size + picked.size], axis=0)


def contract_rows(block_rows, both_logits):
    return lax.dot_general(
        block_rows, both_logits, (((0,), (0,)), ((), ())), preferred_element_type=jnp.float32
    )


def shards(hidden, head_weight, token_ids, response_mask, pair_order, frozen_logprob):
    seqs, local, width = hidden.shape
    rows = seqs * local
    block = jnp.concatenate([hidden.reshape(rows, width), to_planes(token_ids, response_mask)])
    blocks = lax.all_gather(block, "ctx", axis=0)
    ctx_count = blocks.shape[0]
    token_rows = blocks[:, :rows].reshape(ctx_count * rows, width)
    planes = blocks[:, rows:].reshape(ctx_count, 4, rows)
    ids_flat, mask_flat = from_planes(jnp.moveaxis(planes, 1, 0).reshape(4, -1))
    shard_width = head_weight.shape[1]
    whole_rows = lax.all_gather(token_rows, VOCAB, axis=1, tiled=True)
    logits = jnp.dot(whole_rows, head_weight, preferred_element_type=jnp.float32)
    offset = lax.axis_index(CTX_VOCAB) * shard_width
    local_ids = ids_flat - offset
    columns = jnp.arange(shard_width).astype(jnp.int32)
    hit = columns[None, :] == local_ids[:, None]
    picked_part = jnp.sum(jnp.where(hit, logits, 0.0), axis=1)
    peak = jnp.max(logits, axis=1)
    lse = peak + jnp.log(jnp.sum(jnp.exp(logits - peak[:, None]), axis=1))
    by_seq = (picked_part * mask_flat).reshape(ctx_count, seqs, local).sum(axis=(0, 2))
    lse, by_seq = exchange(lse, by_seq, VOCAB, 32)
    log_norm, picked = exchange(lse, by_seq, "ctx", ctx_count)
    norm_seq = (log_norm * mask_flat).reshape(ctx_count, seqs, local).sum(axis=(0, 2))
    policy = picked - norm_seq
    log_ratio = policy - frozen_logprob
    pair_count = pair_order.shape[0] // 2
    seq_ids = jnp.arange(seqs)
    is_chosen = (pair_order[:pair_count, None] == seq_ids[None, :]).astype(jnp.float32)
    is_rejected = (pair_order[pair_count:, None] == seq_ids[None, :]).astype(jnp.float32)
    margins = strength * (
        jnp.sum(is_chosen * log_ratio[None], axis=1) - jnp.sum(is_rejected * log_ratio[None], axis=1)
    )
    pair_loss = jnp.mean(jax.nn.softplus(-margins))
    weight = -loss_scale * strength * jax.nn.sigmoid(-margins) / pair_count
    seq_coef = jnp.sum(weight[:, None] * (is_chosen - is_rejected), axis=0)
    token_coef = mask_flat * jnp.broadcast_to(
        seq_coef[None, :, None], (ctx_count, seqs, local)
    ).reshape(-1)
    probabilities = jnp.exp(logits - log_norm[:, None])
    onehot = hit.astype(jnp.float32)
    grad_logits = (token_coef[:, None] * (onehot - probabilities)).astype(jnp.bfloat16)
    spread_logits = (V / 64.0 * token_coef[:, None] * probabilities).astype(jnp.bfloat16)
    both_logits = jnp.concatenate([grad_logits, spread_logits], axis=1)
    both_grads = contract_rows(whole_rows, both_logits)
    head_grad = both_grads[:, :shard_width].astype(jnp.bfloat16)
    spread_grad = both_grads[:, shard_width:].astype(jnp.bfloat16)
    return (pair_loss, margins, head_grad, spread_grad)


def solution(mesh):
    split = Mesh(
        mesh.devices.reshape(mesh.shape["ctx"], 4, 4, 2), ("ctx", "vocab_0", "vocab_1", "vocab_2")
    )
    placed = (P(None, "ctx", VOCAB), P(None, CTX_VOCAB), P(None, "ctx"), P(None, "ctx"), P(), P())
    return jax.shard_map(
        shards,
        mesh=split,
        in_specs=placed,
        out_specs=(P(), P(), P(None, CTX_VOCAB), P(None, CTX_VOCAB)),
        check_vma=False,
    )
```

time: 282 us -> 210 us (0.74)
  blocking collectives: 144 us -> 23.8 us
  waiting for transfers between devices: 68.8 us -> 107 us
  starting transfers between devices: 0.04 us -> 12.9 us
    psum x4 -> x0, blocking collectives: 60.1 us -> none  [by_axis_2(): shard = lax.psum(shard, axis)]
    pmax x4 -> x0, blocking collectives: 39.7 us -> none  [by_axis(): shard = lax.pmax(shard, axis)]
    all_gather x1, waiting for transfers between devices: 68.8 us -> 89.9 us  [shards(): whole_rows = lax.all_gather(token_rows, VOCAB, axis=1, tiled=True)]
    all_gather x2 -> x1, blocking collectives: 44.6 us -> 23.8 us  [shards(): blocks = lax.all_gather(block, 'ctx', axis=0)]
    all_to_all x0 -> x2, waiting for transfers between devices: none -> 17.3 us  [exchange(): lax.all_to_all(jnp.broadcast_to(block[None], (count, *block.shape)), axes...]
    all_to_all x0 -> x2, starting transfers between devices: none -> 12.8 us  [exchange(): lax.all_to_all(jnp.broadcast_to(block[None], (count, *block.shape)), axes...]
  transfers between devices with their start and end apart: 1 -> 3, of which waited for: 1 -> 3; matrix products, arithmetic and copies ran while one was open for 1% -> 0% of each run, Pallas kernels for 0% -> 0%
where the time goes in v1:
time: 210 us
  waiting for transfers between devices  107 us (51%)
  matrix products  33.2 us (16%)
  blocking collectives  23.8 us (11%)
  between operations  16 us (8%)
  starting transfers between devices  12.9 us (6%)
  local copies, waits for them, and re-layouts  9.19 us (4%)
  other arithmetic  7.61 us (4%)
    all_gather x1, waiting for transfers between devices, shards(): whole_rows = lax.all_gather(token_rows, VOCAB, axis=1, tiled=True)  89.9 us
    all_gather x1, blocking collectives, shards(): blocks = lax.all_gather(block, 'ctx', axis=0)  23.8 us
    dot_general x1, matrix products, contract_rows(): lax.dot_general(block_rows, both_logits, (((0,), (0,)), ((), ())), prefer...  20.3 us
    all_to_all x2, waiting for transfers between devices, exchange(): lax.all_to_all(jnp.broadcast_to(block[None], (count, *block.shape)), axes...  17.3 us
    dot_general x1, matrix products, shards(): jnp.dot(whole_rows, head_weight, preferred_element_type=jnp.float32)  12.9 us
    all_to_all x2, starting transfers between devices, exchange(): lax.all_to_all(jnp.broadcast_to(block[None], (count, *block.shape)), axes...  12.8 us
  transfers between devices with their start and end apart: 3, of which 3 were waited for; matrix products, arithmetic and copies ran while one was open for 0% of the time, Pallas kernels for 0%

profile of v1, /device:TPU:1, one launch (start us, length us, event | category | flops | bytes accessed | tf_op | source)
XLA Modules:
  0.0 209.9 jit_solution(10015502931736395149)
XLA Ops:
  7.2 0.7 fusion.3
  7.9 0.1 convert_element_type.66
  8.0 0.8 pad_maximum_fusion
  8.9 23.8 %all-gather = bf16[2112,128]{1,0:T(8,128)(2,1)S(1)} all-gather(bf16[264,128]{1,0:T(8,128)(2,1)S(1)} %pad_maximum_fusion), channel_id=2, replica_groups=mesh['ctx'=8,'vocab_0'=4,'vocab_1'=4,'vocab_2'=2] {'ctx'}, dimensions={0}, use_global_device_ids=true | all-gather | bytes 608256 | tf_op jit(solution)/shard_map/all_gather | solution.py:49
  32.7 0.8 slice.46
  33.7 89.9 %all-gather.3.cloned.1.call-done = bf16[2048,4096]{1,0:T(8,128)(2,1)} async-done(((bf16[2048,128]{1,0:T(8,128)(2,1)}), bf16[2048,4096]{1,0:T(8,128)(2,1)}) %all-gather.3.cloned.1.call-update) | async-done | bytes 16777232 | tf_op jit(solution)/shard_map/all_gather | solution.py:55
  123.6 12.9 %fusion.11 = (f32[2048]{0:T(1024)S(1)}, f32[2048,501]{0,1:T(8,128)S(1)}) fusion(bf16[2048,4096]{1,0:T(8,128)(2,1)} %all-gather.3.cloned.1.call-done, bf16[4096,501]{0,1:T(8,128)(2,1)} %param.7), kind=kOutput, calls=%fused_computation.50 | convolution fusion | flops 8406409216 | bytes 24993792 | tf_op jit(solution)/shard_map/dot_general | solution.py:56
  136.5 2.0 copy-done
  138.5 1.1 select_reduce_fusion
  139.7 0.1 multiply_reduce_fusion.1
  139.9 0.8 broadcast_in_dim.16
  140.7 6.1 %all-to-all-start = ((f32[32,17,128]{2,1,0:T(8,128)}), f32[32,17,128]{2,1,0:T(8,128)S(1)}, u32[]{:S(2)}, u32[]{:S(2)}) async-start(f32[32,17,128]{2,1,0:T(8,128)} %broadcast_in_dim.16), calls=%async_computation | async-start | bytes 786432 | tf_op jit(solution)/shard_map/all_to_all | solution.py:29
  146.8 10.1 %all-to-all-done = f32[32,17,128]{2,1,0:T(8,128)S(1)} async-done(((f32[32,17,128]{2,1,0:T(8,128)}), f32[32,17,128]{2,1,0:T(8,128)S(1)}, u32[]{:S(2)}, u32[]{:S(2)}) %all-to-all-start) | async-done | bytes 278560 | tf_op jit(solution)/shard_map/all_to_all | solution.py:29
  157.2 0.7 broadcast_in_dim.18
  157.8 6.7 %all-to-all-start.1 = ((f32[8,17,128]{2,1,0:T(8,128)}), f32[8,17,128]{2,1,0:T(8,128)S(1)}, u32[]{:S(2)}, u32[]{:S(2)}) async-start(f32[8,17,128]{2,1,0:T(8,128)} %broadcast_in_dim.18), calls=%async_computation.1 | async-start | bytes 196608 | tf_op jit(solution)/shard_map/all_to_all | solution.py:29
  164.7 7.2 %all-to-all-done.1 = f32[8,17,128]{2,1,0:T(8,128)S(1)} async-done(((f32[8,17,128]{2,1,0:T(8,128)}), f32[8,17,128]{2,1,0:T(8,128)S(1)}, u32[]{:S(2)}, u32[]{:S(2)}) %all-to-all-start.1) | async-done | bytes 69664 | tf_op jit(solution)/shard_map/all_to_all | solution.py:29
  172.1 0.1 multiply_reduce_fusion
  172.2 0.2 select_reduce_fusion.1
  172.4 0.1 multiply_reduce_fusion.2
  172.6 0.1 reshape.128
  172.7 3.5 %multiply_convert_fusion.1 = (bf16[2048,501]{0,1:T(8,128)(2,1)S(1)}, bf16[2048,501]{0,1:T(8,128)(2,1)S(1)}) fusion(f32[2048,501]{0,1:T(8,128)} %copy-done, f32[2048]{0:T(1024)S(1)} %log_add_fusion, f32[2048]{0:T(1024)S(1)} %get-tuple-element.9, s32[2048]{0:T(1024)S(1)} %bitcast.45, f32[2048]{0:T(1024)S(1)} %get-tuple-element.8), kind=kLoop, calls=%fused_computation.5 | loop fusion | flops 8208384 | bytes 8241152 | tf_op jit(solution)/shard_map/convert_element_type | solution.py:85
  176.2 20.3 %convolution_convert_fusion = bf16[4096,1002]{0,1:T(8,128)(2,1)S(1)} fusion(bf16[2048,4096]{1,0:T(8,128)(2,1)} %all-gather.3.cloned.1.call-done, bf16[2048,501]{0,1:T(8,128)(2,1)S(1)} %get-tuple-element.15, bf16[2048,501]{0,1:T(8,128)(2,1)S(1)} %get-tuple-element.14), kind=kOutput, calls=%fused_computation | convolution fusion | flops 16823083008 | bytes 29089792 | tf_op jit(solution)/shard_map/dot_general | solution.py:40
  196.6 4.1 %fusion.9 = (bf16[4096,501]{0,1:T(8,128)(2,1)}, bf16[4096,501]{0,1:T(8,128)(2,1)}) fusion(bf16[4096,1002]{0,1:T(8,128)(2,1)S(1)} %convolution_convert_fusion), kind=kLoop, calls=%fused_computation.48 | loop fusion | bytes 16416768 | tf_op jit(solution)/shard_map/slice | solution.py:90
  200.7 0.6 fusion.7
  (39 shorter events, 1.0 us)
Async XLA Ops:
  7.2 116.5 %all-gather.3.cloned.1.call-start = ((), (), s32[]{:S(2)}) async-start(), calls=%async_computation.2 | async-start | bytes 17301504 | tf_op jit(solution)/shard_map/all_gather | solution.py:55
  136.5 2.0 copy-start
  136.5 28.1 %copy-start.1 = (s32[16]{0:T(128)S(1)}, s32[16]{0:T(128)}, u32[]{:S(2)}) copy-start(s32[16]{0:T(128)} %param.10) | copy-start | bytes 196
  136.5 35.6 %copy-start.2 = (f32[16]{0:T(128)S(1)}, f32[16]{0:T(128)}, u32[]{:S(2)}) copy-start(f32[16]{0:T(128)} %param.11) | copy-start | bytes 196
  140.7 16.3 %all-to-all-start = ((f32[32,17,128]{2,1,0:T(8,128)}), f32[32,17,128]{2,1,0:T(8,128)S(1)}, u32[]{:S(2)}, u32[]{:S(2)}) async-start(f32[32,17,128]{2,1,0:T(8,128)} %broadcast_in_dim.16), calls=%async_computation | async-start | bytes 786432 | tf_op jit(solution)/shard_map/all_to_all | solution.py:29
  157.8 14.0 %all-to-all-start.1 = ((f32[8,17,128]{2,1,0:T(8,128)}), f32[8,17,128]{2,1,0:T(8,128)S(1)}, u32[]{:S(2)}, u32[]{:S(2)}) async-start(f32[8,17,128]{2,1,0:T(8,128)} %broadcast_in_dim.18), calls=%async_computation.1 | async-start | bytes 196608 | tf_op jit(solution)/shard_map/all_to_all | solution.py:29
  172.4 28.3 %copy-start.3 = (f32[8]{0:T(128)}, f32[8]{0:T(128)S(1)}, u32[]{:S(2)}) copy-start(f32[8]{0:T(128)S(1)} %get-tuple-element.11) | copy-start | bytes 100
Sparse Core Ops, SparseCore 0:
  33.6 89.9 all-gather.2
